TPU v7x, 32 devices: a whole 2x2x4 slice. The times are simulated.
32 devices in a mesh: fsdp: 8 (over z, y), seq: 4 (over x, core).
Axes of the slice: x: 2, y: 2, z: 4, core: 2. Of those that a mesh axis runs over, the one named last changes fastest.
Arguments:
- tokens: bfloat16 [8, 512, 4096], P('fsdp'), may hold values from -7 to 7
- norm_gain: float32 [4096], replicated, may hold values from 0.1 to 1.9
- curvature: bfloat16 [8, 512, 4096], P('fsdp'), may hold values from 0.19921875 to 2
- weight_slots: bfloat16 [4, 400, 128, 128], P('seq', 'fsdp'), may hold values from -1 to 1
- probe_slots: bfloat16 [4, 400, 128, 128], P('seq', 'fsdp'), may hold values from -0.09375 to 0.09375
- block_counts: int32 [4, 8], P('seq'), may hold values from 1 to 50, 320 in all within a row
Outputs:
- hvp_slots: float32 [4, 400, 128, 128], P('seq', 'fsdp')
Inputs may be any that keep to these rules, and one draw needn't show every extreme that they name: `block_counts`: in each row, device d along fsdp owns the n_d blocks that follow the earlier devices' blocks, in its first n_d slots; a row sums to 320, and 50 is reached in every row.
All inputs are finite; a program needn't handle non-finite values.
Results may differ from a plain program's by a relative error of at most 0.018.
Values may be sent and summed in bfloat16 or wider, within the bound.
A program may use at most 128 MiB of HBM per device.

v0:
```python
import jax
import jax.numpy as jnp
from jax import lax
from jax.sharding import PartitionSpec as P

D = 4096
HQ = 16
HK = 4
HD = 128
BLK = 128


THETA = 500000.0
EPS = 1e-05
NEGATIVE = -1e30


def rotary(length, head_dim):
    half_dim = head_dim // 2
    frequency = jnp.exp(-jnp.log(THETA) * 2.0 * jnp.arange(half_dim, dtype=jnp.float32) / head_dim)
    angles = jnp.arange(length, dtype=jnp.float32)[:, None] * frequency[None, :]
    return (jnp.cos(angles)[:, None, :], jnp.sin(angles)[:, None, :])


def rotate(field_in, cosine, sine):
    half_dim = field_in.shape[-1] // 2
    first_half = field_in[..., :half_dim]
    second = field_in[..., half_dim:]
    return jnp.concatenate(
        [first_half * cosine - second * sine, second * cosine + first_half * sine], axis=-1
    )


def attention_branch(w_qkv, w_out, normed, cosine, sine, q_heads, kv_heads):
    length = normed.shape[0]
    head_dim = w_out.shape[0] // q_heads
    projected = jnp.dot(normed, w_qkv, preferred_element_type=jnp.float32)
    q_end = q_heads * head_dim
    k_end = q_end + kv_heads * head_dim
    queries = rotate(projected[:, :q_end].reshape(length, q_heads, head_dim), cosine, sine).astype(
        jnp.bfloat16
    )
    key_rows = rotate(
        projected[:, q_end:k_end].reshape(length, kv_heads, head_dim), cosine, sine
    ).astype(jnp.bfloat16)
    values = projected[:, k_end:].reshape(length, kv_heads, head_dim).astype(jnp.bfloat16)
    queries = queries.reshape(length, kv_heads, q_heads // kv_heads, head_dim)
    scores = jnp.einsum(
        "qkgd,skd->kgqs", queries, key_rows, preferred_element_type=jnp.float32
    ) * head_dim ** (-0.5)
    causal = jnp.arange(length)[:, None] >= jnp.arange(length)[None, :]
    scores = jnp.where(causal, scores, NEGATIVE)
    attn_probs = jax.nn.softmax(scores, axis=-1).astype(jnp.bfloat16)
    mixed_heads = jnp.einsum(
        "kgqs,skd->qkgd", attn_probs, values, preferred_element_type=jnp.float32
    )
    mixed_heads = mixed_heads.reshape(length, q_heads * head_dim).astype(jnp.bfloat16)
    return jnp.dot(mixed_heads, w_out, preferred_element_type=jnp.float32)


def to_matrix(blocks, row_blocks, col_blocks):
    blk_edge = blocks.shape[-1]
    return (
        blocks.reshape(row_blocks, col_blocks, blk_edge, blk_edge)
        .transpose(0, 2, 1, 3)
        .reshape(row_blocks * blk_edge, col_blocks * blk_edge)
    )


def to_blocks(matrix, blk_edge):
    row_blocks = matrix.shape[0] // blk_edge
    col_blocks = matrix.shape[1] // blk_edge
    return (
        matrix.reshape(row_blocks, blk_edge, col_blocks, blk_edge)
        .transpose(0, 2, 1, 3)
        .reshape(row_blocks * col_blocks, blk_edge, blk_edge)
    )


def local(tokens, norm_gain, curvature, weight_slots, probe_slots, block_counts):
    n_columns = lax.axis_size("seq")
    n_owners = lax.axis_size("fsdp")
    q_heads = HQ // n_columns
    kv_heads = HK // n_columns
    row_blocks = D // BLK
    qkv_cols = (q_heads + 2 * kv_heads) * HD // BLK
    out_rows = q_heads * HD // BLK
    qkv_split = row_blocks * qkv_cols
    total_blocks = qkv_split + out_rows * row_blocks
    slots = weight_slots.shape[1]
    length = tokens.shape[1]
    counts = block_counts[0]
    range_ends = jnp.cumsum(counts)
    starts = range_ends - counts
    owner_ids = jnp.arange(n_owners, dtype=jnp.int32)
    gathered_w, gathered_p = (
        lax.all_gather(weight_slots[0], "fsdp", axis=0, tiled=True),
        lax.all_gather(probe_slots[0], "fsdp", axis=0, tiled=True),
    )
    block_ids = jnp.arange(total_blocks, dtype=jnp.int32)
    owners = jnp.sum((range_ends[None, :] <= block_ids[:, None]).astype(jnp.int32), axis=1)
    first_block = jnp.sum(
        jnp.where(owners[:, None] == owner_ids[None, :], starts[None, :], 0), axis=1
    )
    slot_of = owners * slots + block_ids - first_block
    w_blocks = gathered_w[slot_of]
    p_blocks = gathered_p[slot_of]
    w_qkv = to_matrix(w_blocks[:qkv_split], row_blocks, qkv_cols)
    w_out = to_matrix(w_blocks[qkv_split:], out_rows, row_blocks)
    p_qkv = to_matrix(p_blocks[:qkv_split], row_blocks, qkv_cols)
    p_out = to_matrix(p_blocks[qkv_split:], out_rows, row_blocks)
    values = tokens[0].astype(jnp.float32)
    factor = lax.rsqrt(jnp.mean(values * values, axis=-1, keepdims=True) + EPS)
    normed = (values * factor * norm_gain).astype(jnp.bfloat16)
    cosine, sine = rotary(length, HD)

    def inner(first_w, second_w):
        return attention_branch(first_w, second_w, normed, cosine, sine, q_heads, kv_heads)

    _, tangent = jax.jvp(inner, (w_qkv, w_out), (p_qkv, p_out))
    share = lax.psum_scatter(
        tangent.astype(jnp.bfloat16), "seq", scatter_dimension=1, tiled=True
    ).astype(jnp.float32)
    share_width = share.shape[1]
    curv_share = lax.dynamic_slice_in_dim(
        curvature[0], lax.axis_index("seq") * share_width, share_width, 1
    )
    weighted_share = (curv_share.astype(jnp.float32) * share).astype(jnp.bfloat16)
    weighted = lax.all_gather(weighted_share, "seq", axis=1, tiled=True)
    _, pullback = jax.vjp(inner, w_qkv, w_out)
    g_qkv, g_out = pullback(weighted.astype(jnp.float32))
    grad_blocks = jnp.concatenate([to_blocks(g_qkv, BLK), to_blocks(g_out, BLK)], axis=0)
    slot_index = jnp.arange(lax.axis_size("fsdp") * slots, dtype=jnp.int32)
    slot_owner = slot_index // slots
    slot_place = slot_index % slots
    owner_hot = slot_owner[:, None] == owner_ids[None, :]
    owner_first = jnp.sum(jnp.where(owner_hot, starts[None, :], 0), axis=1)
    own_count = jnp.sum(jnp.where(owner_hot, counts[None, :], 0), axis=1)
    is_live = slot_place < own_count
    picked = jnp.clip(owner_first + slot_place, 0, total_blocks - 1)
    summed_slots = lax.psum_scatter(
        jnp.where(is_live[:, None, None], grad_blocks[picked].astype(jnp.float32), 0.0).astype(
            jnp.bfloat16
        ),
        "fsdp",
        scatter_dimension=0,
        tiled=True,
    ).astype(jnp.float32)
    scaled = summed_slots * (1.0 / jnp.sqrt(jnp.float32(length * n_owners)))
    return scaled.reshape(1, slots, BLK, BLK)


def solution(mesh):
    in_specs = (
        P("fsdp", None, None),
        P(),
        P("fsdp", None, None),
        P("seq", "fsdp", None, None),
        P("seq", "fsdp", None, None),
        P("seq", None),
    )
    out_specs = P("seq", "fsdp", None, None)
    return jax.shard_map(local, mesh=mesh, in_specs=in_specs, out_specs=out_specs, check_vma=False)
```

profile of v0, /device:TPU:0, one launch (start us, length us, event | category | flops | bytes accessed | tf_op | source)
XLA Modules:
  0.0 873.3 jit_solution(1264683456025158661)
XLA Ops:
  15.2 179.5 %all-gather.8.cloned.1.call-done = bf16[1,400,128,128]{3,2,0,1:T(8,128)(2,1)} async-done(((bf16[1,50,128,128]{3,2,0,1:T(8,128)(2,1)}), bf16[1,400,128,128]{3,2,0,1:T(8,128)(2,1)}) %all-gather.8.cloned.1.call-update) | async-done | bytes 13107216 | tf_op jit(solution)/shard_map/all_gather | solution.py:98
  194.8 15.4 %gather_fusion = bf16[320,128,128]{2,1,0:T(8,128)(2,1)} fusion(bf16[400,128,128]{2,1,0:T(8,128)(2,1)} %bitcast.284, s32[1024]{0:T(1024)S(1)} %pad_clamp_fusion.1), kind=kCustom, calls=%fused_computation | custom fusion | bytes 20972800 | tf_op jit(solution)/shard_map/gather | solution.py:107
  210.1 8.1 slice.87
  218.2 159.5 %all-gather.10.cloned.1.call-done = bf16[1,400,128,128]{3,2,0,1:T(8,128)(2,1)} async-done(((bf16[1,50,128,128]{3,2,0,1:T(8,128)(2,1)}), bf16[1,400,128,128]{3,2,0,1:T(8,128)(2,1)}) %all-gather.10.cloned.1.call-update) | async-done | bytes 13107216 | tf_op jit(solution)/shard_map/all_gather | solution.py:97
  377.7 15.5 %gather_fusion.1 = bf16[320,128,128]{2,1,0:T(8,128)(2,1)} fusion(bf16[400,128,128]{2,1,0:T(8,128)(2,1)} %bitcast.285, s32[1024]{0:T(1024)S(1)} %pad_clamp_fusion.1), kind=kCustom, calls=%fused_computation.1 | custom fusion | bytes 20972800 | tf_op jit(solution)/shard_map/gather | solution.py:106
  393.1 8.1 slice.89
  401.2 9.1 %copy.75 = bf16[32,6,128,128]{2,0,3,1:T(8,128)(2,1)} copy(bf16[32,6,128,128]{3,2,1,0:T(8,128)(2,1)} %bitcast.274) | data formatting | bytes 12582912 | tf_op jit(solution)/shard_map/reshape | solution.py:64
  410.3 8.4 fusion.10
  420.0 8.9 %copy.77 = bf16[32,6,128,128]{2,0,3,1:T(8,128)(2,1)} copy(bf16[32,6,128,128]{3,2,1,0:T(8,128)(2,1)} %bitcast.275) | data formatting | bytes 12582912 | tf_op jit(solution)/shard_map/reshape | solution.py:64
  428.9 8.3 fusion.7
  466.6 4.7 add_convert_fusion
  471.4 42.7 %reduce-scatter.3.cloned.1.call-done = bf16[512,1024]{1,0:T(8,128)(2,1)} async-done(((bf16[512,4096]{1,0:T(8,128)(2,1)}), bf16[512,1024]{1,0:T(8,128)(2,1)}) %reduce-scatter.3.cloned.1.call-update) | async-done | bytes 1048592 | tf_op jit(solution)/shard_map/reduce_scatter | solution.py:121
  519.1 32.5 %all-gather.6.cloned.1.call-done = bf16[512,4096]{1,0:T(8,128)(2,1)} async-done(((bf16[512,1024]{1,0:T(8,128)(2,1)}), bf16[512,4096]{1,0:T(8,128)(2,1)}) %all-gather.6.cloned.1.call-update) | async-done | bytes 4194320 | tf_op jit(solution)/shard_map/all_gather | solution.py:129
  551.6 6.1 fusion.57
  569.3 3.9 copy.99
  576.5 5.6 convolution_convert_fusion
  582.1 8.7 copy.97
  590.8 7.5 copy.127
  598.3 9.2 %copy.98 = bf16[32,6,128,128]{3,2,1,0:T(8,128)(2,1)} copy(bf16[32,6,128,128]{2,0,3,1:T(8,128)(2,1)} %bitcast.277) | data formatting | bytes 12582912 | tf_op jit(solution)/shard_map/transpose | solution.py:75
  607.5 11.5 %pad_maximum_fusion = bf16[320,128,128]{2,1,0:T(8,128)(2,1)} fusion(bf16[128,128,128]{2,1,0:T(8,128)(2,1)} %bitcast.281, bf16[192,128,128]{2,1,0:T(8,128)(2,1)} %bitcast.278), kind=kLoop, calls=%fused_computation.8 | loop fusion | flops 5242880 | bytes 20971520 | tf_op jit(solution)/shard_map/concatenate | solution.py:132
  619.0 16.8 %gather_fusion.2 = bf16[400,128,128]{2,1,0:T(8,128)(2,1)} fusion(bf16[320,128,128]{2,1,0:T(8,128)(2,1)} %pad_maximum_fusion, s32[1024]{0:T(1024)S(1)} %copy-done.14), kind=kCustom, calls=%fused_computation.2 | custom fusion | bytes 26216000 | tf_op jit(solution)/shard_map/gather | solution.py:142
  635.9 11.9 %select_convert_fusion = bf16[400,128,128]{2,1,0:T(8,128)(2,1)} fusion(bf16[400,128,128]{2,1,0:T(8,128)(2,1)} %gather_fusion.2, pred[400]{0:T(512)(128)(4,1)S(1)} %copy-done.19), kind=kLoop, calls=%fused_computation.3 | loop fusion | flops 19660800 | bytes 26214800 | tf_op jit(solution)/shard_map/convert_element_type | solution.py:142
  647.8 215.0 %reduce-scatter.5.cloned.1.call-done = bf16[50,128,128]{2,1,0:T(8,128)(2,1)} async-done(((bf16[400,128,128]{2,1,0:T(8,128)(2,1)}), bf16[50,128,128]{2,1,0:T(8,128)(2,1)}) %reduce-scatter.5.cloned.1.call-update) | async-done | bytes 1638416 | tf_op jit(solution)/shard_map/reduce_scatter | solution.py:141
  862.8 3.5 multiply_bitcast_fusion
  (116 shorter events, 58.9 us)
Async XLA Ops:
  6.5 188.2 %all-gather.8.cloned.1.call-start = ((), (), s32[]{:S(2)}) async-start(), calls=%async_computation.5 | async-start | bytes 14745600 | tf_op jit(solution)/shard_map/all_gather | solution.py:98
  7.3 370.4 %all-gather.10.cloned.1.call-start = ((), (), s32[]{:S(2)}) async-start(), calls=%async_computation.6 | async-start | bytes 14745600 | tf_op jit(solution)/shard_map/all_gather | solution.py:97
  8.0 506.0 %reduce-scatter.3.cloned.1.call-start = ((), (), s32[]{:S(2)}) async-start(), calls=%async_computation.2 | async-start | bytes 5242880 | tf_op jit(solution)/shard_map/reduce_scatter | solution.py:121
  10.3 429.9 %copy-start.17 = (f32[64]{0:T(128)}, f32[64]{0:T(128)S(1)}, u32[]{:S(2)}) copy-start(f32[64]{0:T(128)S(1)} %multiply_exponential_fusion) | copy-start | bytes 772
  13.5 415.4 %copy-start.21 = (f32[512]{0:T(512)}, f32[512]{0:T(512)S(1)}, u32[]{:S(2)}) copy-start(f32[512]{0:T(512)S(1)} %add_rsqrt_fusion) | copy-start | bytes 6148
  401.2 9.1 %copy-start.24 = (f32[4096]{0:T(1024)S(1)}, f32[4096]{0:T(1024)}, u32[]{:S(2)}) copy-start(f32[4096]{0:T(1024)} %param.7) | copy-start | bytes 49156
  442.9 12.9 %copy-start.12 = (bf16[512,64]{1,0:T(8,128)(2,1)}, bf16[512,64]{1,0:T(8,128)(2,1)S(1)}, u32[]{:S(2)}) copy-start(bf16[512,64]{1,0:T(8,128)(2,1)S(1)} %get-tuple-element.26) | copy-start | bytes 196612
  445.9 13.7 %copy-start = (f32[512,512,4]{1,0,2:T(8,128)}, f32[512,512,4]{1,0,2:T(8,128)S(1)}, u32[]{:S(2)}) copy-start(f32[512,512,4]{1,0,2:T(8,128)S(1)} %get-tuple-element.30) | copy-start | bytes 12582916
  446.8 2.7 slice-start.1
  446.8 12.7 %copy-start.15 = (f32[4,512]{1,0:T(4,128)}, f32[4,512]{1,0:T(4,128)S(1)}, u32[]{:S(2)}) copy-start(f32[4,512]{1,0:T(4,128)S(1)} %multiply_divide_fusion) | copy-start | bytes 24580
  449.5 2.7 slice-start
  454.9 9.1 %copy-start.2 = (bf16[4,32,128,128]{3,1,2,0:T(8,128)(2,1)}, bf16[4,32,128,128]{3,1,2,0:T(8,128)(2,1)S(1)}, u32[]{:S(2)}) copy-start(bf16[4,32,128,128]{3,1,2,0:T(8,128)(2,1)S(1)} %copy.86) | copy-start | bytes 12582916
  459.5 7.1 copy-start.4
  471.3 80.3 %all-gather.6.cloned.1.call-start = ((), (), s32[]{:S(2)}) async-start(), calls=%async_computation.3 | async-start | bytes 5242880 | tf_op jit(solution)/shard_map/all_gather | solution.py:129
  517.0 345.8 %reduce-scatter.5.cloned.1.call-start = ((), (), s32[]{:S(2)}) async-start(), calls=%async_computation.4 | async-start | bytes 14745600 | tf_op jit(solution)/shard_map/reduce_scatter | solution.py:141
  551.6 6.8 copy-start.1
  551.6 6.8 copy-start.16
  563.2 2.4 copy-start.23
  569.2 4.0 copy-start.18
  569.3 5.1 copy-start.7
  569.3 5.1 copy-start.9
  574.3 2.2 copy-start.3
  607.5 11.5 %copy-start.14 = (s32[1024]{0:T(1024)S(1)}, s32[1024]{0:T(1024)}, u32[]{:S(2)}) copy-start(s32[1024]{0:T(1024)} %pad_clamp_fusion) | copy-start | bytes 12292
  619.0 16.9 %copy-start.19 = (pred[400]{0:T(512)(128)(4,1)S(1)}, pred[400]{0:T(512)(128)(4,1)}, u32[]{:S(2)}) copy-start(pred[400]{0:T(512)(128)(4,1)} %fusion.109) | copy-start | bytes 1204
  (9 other events, 14.8 us)
Sparse Core Ops, SparseCore 0:
  9.5 185.2 all-gather.7
  197.0 180.6 all-gather.9
  471.4 42.5 reduce-scatter.2
  517.1 34.4 all-gather.5
  647.9 214.7 reduce-scatter.4
where the time goes:
time: 882 us; the launch traced here: 873 us
  waiting for transfers between devices  631 us (72%)
  local copies, waits for them, and re-layouts  127 us (14%)
  matrix products  55.8 us (6%)
  other arithmetic  45.6 us (5%)
  between operations  14.2 us (2%)
    reduce_scatter x1, waiting for transfers between devices, local(): lax.psum_scatter(jnp.where(is_live[:, None, None], grad_blocks[picked].as...  215 us
    all_gather x1, waiting for transfers between devices, local(): lax.all_gather(probe_slots[0], 'fsdp', axis=0, tiled=True)  180 us
    all_gather x1, waiting for transfers between devices, local(): lax.all_gather(weight_slots[0], 'fsdp', axis=0, tiled=True)  159 us
    reduce_scatter x1, waiting for transfers between devices, local(): lax.psum_scatter(tangent.astype(jnp.bfloat16), 'seq', scatter_dimension=1...  42.7 us
    all_gather x1, waiting for transfers between devices, local(): weighted = lax.all_gather(weighted_share, 'seq', axis=1, tiled=True)  32.5 us
    reshape x4, local copies, waits for them, and re-layouts, to_matrix(): blocks.reshape(row_blocks, col_blocks, blk_edge, blk_edge)  23.4 us
    dot_general x3, matrix products, attention_branch(): projected = jnp.dot(normed, w_qkv, preferred_element_type=jnp.float32)  22.3 us
  transfers between devices with their start and end apart: 5, of which 5 were waited for; matrix products, arithmetic and copies ran while one was open for 4% of the time, Pallas kernels for 0%

commit v1 on v0

v1 whole, which is shorter than its diff:
```python
import functools

import jax
import jax.numpy as jnp
from jax import lax
from jax.experimental import pallas as pl
from jax.experimental.pallas import tpu as pltpu
from jax.sharding import PartitionSpec as P

D = 4096
HQ = 16
HK = 4
HD = 128
BLK = 128


THETA = 500000.0
EPS = 1e-05
NEGATIVE = -1e30


def rotary(length, head_dim):
    half_dim = head_dim // 2
    frequency = jnp.exp(-jnp.log(THETA) * 2.0 * jnp.arange(half_dim, dtype=jnp.float32) / head_dim)
    angles = jnp.arange(length, dtype=jnp.float32)[:, None] * frequency[None, :]
    return (jnp.cos(angles)[:, None, :], jnp.sin(angles)[:, None, :])


def rotate(field_in, cosine, sine):
    half_dim = field_in.shape[-1] // 2
    first_half = field_in[..., :half_dim]
    second = field_in[..., half_dim:]
    return jnp.concatenate(
        [first_half * cosine - second * sine, second * cosine + first_half * sine], axis=-1
    )


VMEM_BYTES = 62 * 1024 * 1024


def attention(projected, cosine, sine, q_heads, kv_heads):
    length = projected.shape[0]
    head_dim = projected.shape[1] // (q_heads + 2 * kv_heads)
    q_end = q_heads * head_dim
    k_end = q_end + kv_heads * head_dim
    queries = rotate(projected[:, :q_end].reshape(length, q_heads, head_dim), cosine, sine).astype(
        jnp.bfloat16
    )
    key_rows = rotate(
        projected[:, q_end:k_end].reshape(length, kv_heads, head_dim), cosine, sine
    ).astype(jnp.bfloat16)
    values = projected[:, k_end:].reshape(length, kv_heads, head_dim).astype(jnp.bfloat16)
    queries = queries.reshape(length, kv_heads, q_heads // kv_heads, head_dim)
    scores = jnp.einsum(
        "qkgd,skd->kgqs", queries, key_rows, preferred_element_type=jnp.float32
    ) * head_dim ** (-0.5)
    causal = jnp.arange(length)[:, None] >= jnp.arange(length)[None, :]
    scores = jnp.where(causal, scores, NEGATIVE)
    attn_probs = jax.nn.softmax(scores, axis=-1).astype(jnp.bfloat16)
    mixed_heads = jnp.einsum(
        "kgqs,skd->qkgd", attn_probs, values, preferred_element_type=jnp.float32
    )
    return mixed_heads.reshape(length, q_heads * head_dim).astype(jnp.bfloat16)


def ring_position(index, n):
    odd = lax.rem(index, 2)
    half = lax.div(index, 2)
    return (1 - odd) * half + odd * (n - 1 - half)


def ring_index(position, n):
    back = lax.div(position, n // 2)
    return (1 - back) * 2 * position + back * (2 * (n - 1 - position) + 1)


def pieces(slots):
    half = slots // 2
    out = []
    for direction, first, count in ((0, 0, half), (1, half, slots - half)):
        cuts = 5 if count % 5 == 0 else 1
        size = count // cuts
        out.append([(first + i * size, size) for i in range(cuts)])
    return out


def enter(neighbours):
    barrier = pltpu.get_barrier_semaphore()
    for neighbour in neighbours:
        pl.semaphore_signal(
            barrier, inc=1, device_id={"fsdp": neighbour}, device_id_type=pl.DeviceIdType.MESH
        )
    pl.semaphore_wait(barrier, len(neighbours))


def gather_kernel(n, slots, grid_qkv, grid_out, slot_ref, w_ref, p_ref, wq_ref, wo_ref, pq_ref,
                  po_ref, held_w, held_p, send_sem, recv_sem):
    me = lax.axis_index("fsdp")
    pos = ring_position(me, n)
    right = ring_index(lax.rem(pos + 1, n), n)
    left = ring_index(lax.rem(pos + n - 1, n), n)
    towards = (right, left)
    enter((left, right))
    parts = pieces(slots)
    arrays = ((w_ref, held_w), (p_ref, held_p))

    def copy(which, step, direction, j):
        own, held = arrays[which]
        first, size = parts[direction][j]
        shift = n - step if direction == 0 else step
        origin = ring_index(lax.rem(pos + shift, n), n)
        there = held.at[pl.ds(origin * slots + first, size)]
        here = own.at[pl.ds(first, size)] if step == 0 else there
        return pltpu.make_async_remote_copy(
            src_ref=here,
            dst_ref=there,
            send_sem=send_sem.at[which, step, direction, j],
            recv_sem=recv_sem.at[which, step, direction, j],
            device_id={"fsdp": towards[direction]},
            device_id_type=pl.DeviceIdType.MESH,
        )

    def arrival(which, step, direction, j):
        first, size = parts[direction][j]
        own, held = arrays[which]
        shift = n - step - 1 if direction == 0 else step + 1
        origin = ring_index(lax.rem(pos + shift, n), n)
        there = held.at[pl.ds(origin * slots + first, size)]
        pltpu.make_async_remote_copy(
            src_ref=there,
            dst_ref=there,
            send_sem=send_sem.at[which, step, direction, j],
            recv_sem=recv_sem.at[which, step, direction, j],
            device_id={"fsdp": towards[direction]},
            device_id_type=pl.DeviceIdType.MESH,
        ).wait_recv()

    def each():
        for j in range(max(len(parts[0]), len(parts[1]))):
            for direction in range(2):
                if j < len(parts[direction]):
                    yield direction, j

    def unpack(which, qkv_ref, out_ref):
        own, held = arrays[which]
        rows, cols = grid_qkv
        edge = held.shape[-1]

        def qkv_row(i, carry):
            for c in range(cols):
                qkv_ref[pl.ds(pl.multiple_of(i * edge, edge), edge), c * edge:(c + 1) * edge] = (
                    held[slot_ref[i * cols + c]]
                )
            return carry

        lax.fori_loop(0, rows, qkv_row, 0)
        out_rows, out_cols = grid_out

        def out_col(i, carry):
            for r in range(out_rows):
                out_ref[r * edge:(r + 1) * edge, pl.ds(pl.multiple_of(i * edge, edge), edge)] = (
                    held[slot_ref[rows * cols + r * out_cols + i]]
                )
            return carry

        lax.fori_loop(0, out_cols, out_col, 0)

    def finish(which, qkv_ref, out_ref):
        own, held = arrays[which]
        for direction, j in each():
            arrival(which, n - 2, direction, j)
        held[pl.ds(me * slots, slots)] = own[...]
        unpack(which, qkv_ref, out_ref)

    sent = []
    for which in range(2):
        for step in range(n - 1):
            for direction, j in each():
                if step > 0:
                    arrival(which, step - 1, direction, j)
                one = copy(which, step, direction, j)
                one.start()
                sent.append(one)
            if which == 1 and step == 0:
                finish(0, wq_ref, wo_ref)
    finish(1, pq_ref, po_ref)
    for one in sent:
        one.wait_send()


def gather_weights(slot_of, weights, probes, n, grid_qkv, grid_out):
    slots, edge, _ = weights.shape
    cuts = max(len(part) for part in pieces(slots))
    qkv = jax.ShapeDtypeStruct((grid_qkv[0] * edge, grid_qkv[1] * edge), jnp.bfloat16)
    out = jax.ShapeDtypeStruct((grid_out[0] * edge, grid_out[1] * edge), jnp.bfloat16)
    vmem = pl.BlockSpec(memory_space=pltpu.VMEM)
    return pl.pallas_call(
        functools.partial(gather_kernel, n, slots, grid_qkv, grid_out),
        out_shape=(qkv, out, qkv, out),
        in_specs=[pl.BlockSpec(memory_space=pltpu.SMEM), vmem, vmem],
        out_specs=(vmem,) * 4,
        scratch_shapes=[
            pltpu.VMEM((n * slots, edge, edge), jnp.bfloat16),
            pltpu.VMEM((n * slots, edge, edge), jnp.bfloat16),
            pltpu.SemaphoreType.DMA((2, n - 1, 2, cuts)),
            pltpu.SemaphoreType.DMA((2, n - 1, 2, cuts)),
        ],
        compiler_params=pltpu.CompilerParams(
            collective_id=0, has_side_effects=True, vmem_limit_bytes=VMEM_BYTES
        ),
    )(slot_of, weights, probes)


def gradient_kernel(grid_qkv, grid_out, slot_ref, normed_ref, d_proj_ref, mixed_t_ref,
                    weighted_ref, out_ref):
    edge = out_ref.shape[-1]
    rows, cols = grid_qkv
    out_rows, out_cols = grid_out
    group = 2

    def clear(i, carry):
        out_ref[i] = jnp.zeros(out_ref.shape[1:], out_ref.dtype)
        return carry

    lax.fori_loop(0, out_ref.shape[0], clear, 0)

    def qkv_rows(i, carry):
        width = group * edge
        left = normed_ref[:, pl.ds(pl.multiple_of(i * width, width), width)]
        block = lax.dot_general(
            left, d_proj_ref[...], (((0,), (0,)), ((), ())), preferred_element_type=jnp.float32
        ).astype(jnp.bfloat16)
        for r in range(group):
            for c in range(cols):
                out_ref[slot_ref[(i * group + r) * cols + c]] = block[
                    r * edge:(r + 1) * edge, c * edge:(c + 1) * edge
                ]
        return carry

    lax.fori_loop(0, rows // group, qkv_rows, 0)

    def out_columns(i, carry):
        width = group * edge
        right = weighted_ref[:, pl.ds(pl.multiple_of(i * width, width), width)]
        block = jnp.dot(
            mixed_t_ref[...], right, preferred_element_type=jnp.float32
        ).astype(jnp.bfloat16)
        for r in range(out_rows):
            for c in range(group):
                out_ref[slot_ref[rows * cols + r * out_cols + i * group + c]] = block[
                    r * edge:(r + 1) * edge, c * edge:(c + 1) * edge
                ]
        return carry

    lax.fori_loop(0, out_cols // group, out_columns, 0)


def gradient_slots(slot_of, normed, d_proj, mixed_t, weighted, total_slots, grid_qkv, grid_out):
    vmem = pl.BlockSpec(memory_space=pltpu.VMEM)
    return pl.pallas_call(
        functools.partial(gradient_kernel, grid_qkv, grid_out),
        out_shape=jax.ShapeDtypeStruct((total_slots, BLK, BLK), jnp.bfloat16),
        in_specs=[pl.BlockSpec(memory_space=pltpu.SMEM)] + [vmem] * 4,
        out_specs=vmem,
        compiler_params=pltpu.CompilerParams(vmem_limit_bytes=VMEM_BYTES),
    )(slot_of, normed, d_proj, mixed_t, weighted)


def reduce_kernel(n, slots, scale, g_ref, out_ref, held, send_sem, recv_sem):
    me = lax.axis_index("fsdp")
    pos = ring_position(me, n)
    right = ring_index(lax.rem(pos + 1, n), n)
    left = ring_index(lax.rem(pos + n - 1, n), n)
    towards = (right, left)
    enter((left, right))
    parts = pieces(slots)

    def own(step, direction, j):
        first, size = parts[direction][j]
        shift = n - 1 - step if direction == 0 else 1 + step
        target = ring_index(lax.rem(pos + shift, n), n)
        return pl.ds(target * slots + first, size)

    def copy(step, direction, j):
        first, size = parts[direction][j]
        here = g_ref.at[own(0, direction, j)] if step == 0 else held.at[step - 1, pl.ds(first, size)]
        return pltpu.make_async_remote_copy(
            src_ref=here,
            dst_ref=held.at[step, pl.ds(first, size)],
            send_sem=send_sem.at[step, direction, j],
            recv_sem=recv_sem.at[step, direction, j],
            device_id={"fsdp": towards[direction]},
            device_id_type=pl.DeviceIdType.MESH,
        )

    def each():
        for j in range(max(len(parts[0]), len(parts[1]))):
            for direction in range(2):
                if j < len(parts[direction]):
                    yield direction, j

    sent = {}
    for step in range(n - 1):
        for direction, j in each():
            first, size = parts[direction][j]
            if step > 0:
                sent[step - 1, direction, j].wait_recv()
                held[step - 1, pl.ds(first, size)] = (
                    held[step - 1, pl.ds(first, size)].astype(jnp.float32)
                    + g_ref[own(step, direction, j)].astype(jnp.float32)
                ).astype(jnp.bfloat16)
            one = copy(step, direction, j)
            one.start()
            sent[step, direction, j] = one
    for direction, j in each():
        first, size = parts[direction][j]
        sent[n - 2, direction, j].wait_recv()
        out_ref[pl.ds(first, size)] = (
            held[n - 2, pl.ds(first, size)].astype(jnp.float32)
            + g_ref[own(n - 1, direction, j)].astype(jnp.float32)
        ) * scale
    for one in sent.values():
        one.wait_send()


def reduce_slots(partial_slots, n, scale):
    total, edge, _ = partial_slots.shape
    slots = total // n
    cuts = max(len(part) for part in pieces(slots))
    vmem = pl.BlockSpec(memory_space=pltpu.VMEM)
    return pl.pallas_call(
        functools.partial(reduce_kernel, n, slots, scale),
        out_shape=jax.ShapeDtypeStruct((slots, edge, edge), jnp.float32),
        in_specs=[vmem],
        out_specs=vmem,
        scratch_shapes=[
            pltpu.VMEM((n - 1, slots, edge, edge), jnp.bfloat16),
            pltpu.SemaphoreType.DMA((n - 1, 2, cuts)),
            pltpu.SemaphoreType.DMA((n - 1, 2, cuts)),
        ],
        compiler_params=pltpu.CompilerParams(
            collective_id=1, has_side_effects=True, vmem_limit_bytes=VMEM_BYTES
        ),
    )(partial_slots)


def local(tokens, norm_gain, curvature, weight_slots, probe_slots, block_counts):
    n_columns = lax.axis_size("seq")
    n_owners = lax.axis_size("fsdp")
    q_heads = HQ // n_columns
    kv_heads = HK // n_columns
    row_blocks = D // BLK
    qkv_cols = (q_heads + 2 * kv_heads) * HD // BLK
    out_rows = q_heads * HD // BLK
    grid_qkv, grid_out = (row_blocks, qkv_cols), (out_rows, row_blocks)
    total_blocks = row_blocks * qkv_cols + out_rows * row_blocks
    slots = weight_slots.shape[1]
    length = tokens.shape[1]
    counts = block_counts[0]
    range_ends = jnp.cumsum(counts)
    starts = range_ends - counts
    owner_ids = jnp.arange(n_owners, dtype=jnp.int32)
    block_ids = jnp.arange(total_blocks, dtype=jnp.int32)
    owners = jnp.sum((range_ends[None, :] <= block_ids[:, None]).astype(jnp.int32), axis=1)
    first_block = jnp.sum(
        jnp.where(owners[:, None] == owner_ids[None, :], starts[None, :], 0), axis=1
    )
    slot_of = (owners * slots + block_ids - first_block).astype(jnp.int32)
    w_qkv, w_out, p_qkv, p_out = gather_weights(
        slot_of, weight_slots[0], probe_slots[0], n_owners, grid_qkv, grid_out
    )
    values = tokens[0].astype(jnp.float32)
    factor = lax.rsqrt(jnp.mean(values * values, axis=-1, keepdims=True) + EPS)
    normed = (values * factor * norm_gain).astype(jnp.bfloat16)
    cosine, sine = rotary(length, HD)

    def inner(projected):
        return attention(projected, cosine, sine, q_heads, kv_heads)

    projected = jnp.dot(normed, w_qkv, preferred_element_type=jnp.float32)
    d_projected = jnp.dot(normed, p_qkv, preferred_element_type=jnp.float32)
    mixed, d_mixed = jax.jvp(inner, (projected,), (d_projected,))
    tangent = jnp.dot(d_mixed, w_out, preferred_element_type=jnp.float32) + jnp.dot(
        mixed, p_out, preferred_element_type=jnp.float32
    )
    share = lax.psum_scatter(
        tangent.astype(jnp.bfloat16), "seq", scatter_dimension=1, tiled=True
    ).astype(jnp.float32)
    share_width = share.shape[1]
    curv_share = lax.dynamic_slice_in_dim(
        curvature[0], lax.axis_index("seq") * share_width, share_width, 1
    )
    weighted_share = (curv_share.astype(jnp.float32) * share).astype(jnp.bfloat16)
    weighted = lax.all_gather(weighted_share, "seq", axis=1, tiled=True)
    mixed_again, pullback = jax.vjp(inner, projected)
    back_mixed = lax.dot_general(
        weighted, w_out, (((1,), (1,)), ((), ())), preferred_element_type=jnp.float32
    ).astype(jnp.bfloat16)
    (back_projected,) = pullback(back_mixed)
    partial_slots = gradient_slots(
        slot_of,
        normed,
        back_projected.astype(jnp.bfloat16),
        mixed_again.T,
        weighted,
        n_owners * slots,
        grid_qkv,
        grid_out,
    )
    scaled = reduce_slots(partial_slots, n_owners, (length * n_owners) ** -0.5)
    return scaled.reshape(1, slots, BLK, BLK)


def solution(mesh):
    in_specs = (
        P("fsdp", None, None),
        P(),
        P("fsdp", None, None),
        P("seq", "fsdp", None, None),
        P("seq", "fsdp", None, None),
        P("seq", None),
    )
    out_specs = P("seq", "fsdp", None, None)
    return jax.shard_map(local, mesh=mesh, in_specs=in_specs, out_specs=out_specs, check_vma=False)
```

time: 882 us -> 590 us (0.67)
  waiting for transfers between devices: 631 us -> 79.3 us
  Pallas kernels: 0 us -> 422 us
  local copies, waits for them, and re-layouts: 127 us -> 8.78 us
  other arithmetic: 45.6 us -> 20.1 us
  matrix products: 55.8 us -> 41.4 us
    pallas_call x0 -> x3, Pallas kernels: none -> 422 us  [the longest x1 265 us: gather_weights(): pl.pallas_call(functools.partial(gather_kernel, n, slots, grid_qkv, grid_...]
    all_gather x2 -> x0, waiting for transfers between devices: 339 us -> none  [the longest x1 180 us: local(): lax.all_gather(probe_slots[0], 'fsdp', axis=0, tiled=True)]
    reduce_scatter x1 -> x0, waiting for transfers between devices: 215 us -> none  [local(): lax.psum_scatter(jnp.where(is_live[:, None, None], grad_blocks[picked].as...]
    gather x3 -> x0, local copies, waits for them, and re-layouts: 47.7 us -> none  [the longest x1 16.8 us: local(): grad_blocks[picked].astype(jnp.float32)]
    reshape x8 -> x3, local copies, waits for them, and re-layouts: 30.1 us -> 1.96 us  [the longest x2 1.92 us: attention(): projected[:, :q_end].reshape(length, q_heads, head_dim)]
    slice x8 -> x2, local copies, waits for them, and re-layouts: 18.1 us -> 1.31 us  [attention(): projected[:, :q_end].reshape(length, q_heads, head_dim)]
    dot_general x17 -> x15, matrix products: 55.8 us -> 41.4 us  [the longest x5 9.2 us: attention(): jnp.einsum('kgqs,skd->qkgd', attn_probs, values, preferred_element_type=j...]
    concatenate x1 -> x0, other arithmetic: 11.5 us -> none  [local(): jnp.concatenate([to_blocks(g_qkv, BLK), to_blocks(g_out, BLK)], axis=0)]
  transfers between devices with their start and end apart: 5 -> 2, of which waited for: 5 -> 2; matrix products, arithmetic and copies ran while one was open for 4% -> 0% of each run, Pallas kernels for 0% -> 0%
where the time goes in v1:
time: 590 us; the launch traced here: 586 us
  Pallas kernels  422 us (72%)
  waiting for transfers between devices  79.3 us (13%)
  matrix products  41.4 us (7%)
  other arithmetic  20.1 us (3%)
  between operations  14.1 us (2%)
  local copies, waits for them, and re-layouts  8.78 us (1%)
    pallas_call x1, Pallas kernels, gather_weights(): pl.pallas_call(functools.partial(gather_kernel, n, slots, grid_qkv, grid_...  265 us
    pallas_call x1, Pallas kernels, reduce_slots(): pl.pallas_call(functools.partial(reduce_kernel, n, slots, scale), out_sha...  134 us
    reduce_scatter x1, waiting for transfers between devices, local(): lax.psum_scatter(tangent.astype(jnp.bfloat16), 'seq', scatter_dimension=1...  44.6 us
    all_gather x1, waiting for transfers between devices, local(): weighted = lax.all_gather(weighted_share, 'seq', axis=1, tiled=True)  34.6 us
    pallas_call x1, Pallas kernels, gradient_slots(): pl.pallas_call(functools.partial(gradient_kernel, grid_qkv, grid_out), ou...  22.7 us
  transfers between devices with their start and end apart: 2, of which 2 were waited for; matrix products, arithmetic and copies ran while one was open for 0% of the time, Pallas kernels for 0%

profile of v1, /device:TPU:0, one launch (start us, length us, event | category | flops | bytes accessed | tf_op | source)
XLA Modules:
  0.0 586.3 jit_solution(165467883844097389)
XLA Ops:
  9.0 3.1 fusion
  12.1 3.6 fusion.2.normed_ref
  15.6 265.3 %shard_map.64 = (bf16[4096,768]{1,0:T(8,128)(2,1)}, bf16[512,4096]{1,0:T(8,128)(2,1)}, bf16[4096,768]{1,0:T(8,128)(2,1)}, bf16[512,4096]{1,0:T(8,128)(2,1)}) custom-call(s32[320]{0:T(512)} %add_subtract_fusion.slot_ref, bf16[50,128,128]{2,1,0:T(8,128)(2,1)} %bitcast.213, bf16[50,128,128]{2,1,0:T(8,128)(2,1)} %bitcast.214), custom_call_target="tpu_custom_call" | custom-call | tf_op jit(solution)/shard_map/pallas_call | solution.py:197
  281.0 7.2 %fusion.90 = f32[512,768]{1,0:T(8,128)S(1)} fusion(bf16[512,4096]{1,0:T(8,128)(2,1)} %fusion.2.normed_ref, bf16[4096,768]{1,0:T(8,128)(2,1)} %get-tuple-element.10), kind=kOutput, calls=%fused_computation.113 | convolution fusion | flops 3221225472 | bytes 12058624 | tf_op jit(solution)/shard_map/dot_general | solution.py:380
  288.4 3.4 fusion.89
  293.7 1.6 reshape.296
  297.5 1.4 fusion.70
  302.5 1.4 fusion.30
  304.8 2.1 fusion.88
  307.0 3.0 fusion.15
  310.0 1.4 fusion.26
  311.4 2.4 fusion.91
  313.8 4.9 add_convert_fusion
  318.8 44.6 %reduce-scatter.2.cloned.1.call-done = bf16[512,1024]{1,0:T(8,128)(2,1)} async-done(((bf16[512,4096]{1,0:T(8,128)(2,1)}), bf16[512,1024]{1,0:T(8,128)(2,1)}) %reduce-scatter.2.cloned.1.call-update) | async-done | bytes 1048592 | tf_op jit(solution)/shard_map/reduce_scatter | solution.py:386
  363.4 2.9 fusion.14
  366.4 34.6 %all-gather.2.cloned.1.call-done.weighted_ref = bf16[512,4096]{1,0:T(8,128)(2,1)} async-done(((bf16[512,1024]{1,0:T(8,128)(2,1)}), bf16[512,4096]{1,0:T(8,128)(2,1)}) %all-gather.2.cloned.1.call-update) | async-done | bytes 4194320 | tf_op jit(solution)/shard_map/all_gather | solution.py:394
  401.0 6.0 %convolution_convert_fusion.1 = bf16[512,512]{0,1:T(8,128)(2,1)S(1)} fusion(bf16[512,4096]{1,0:T(8,128)(2,1)} %all-gather.2.cloned.1.call-done.weighted_ref, bf16[512,4096]{1,0:T(8,128)(2,1)} %get-tuple-element.11), kind=kOutput, calls=%fused_computation.38 | convolution fusion | flops 2147745792 | bytes 8912896 | tf_op jit(solution)/shard_map/dot_general | solution.py:396
  407.7 2.7 fusion.11
  410.4 2.1 fusion.54
  412.6 2.1 fusion.29
  414.7 1.4 multiply_add_fusion.3
  418.0 22.7 %shard_map.65.g_ref = bf16[400,128,128]{2,1,0:T(8,128)(2,1)} custom-call(s32[320]{0:T(512)} %add_subtract_fusion.slot_ref, bf16[512,4096]{1,0:T(8,128)(2,1)} %fusion.2.normed_ref, bf16[512,768]{1,0:T(8,128)(2,1)} %add_convert_fusion.3.d_proj_ref, bf16[512,512]{1,0:T(8,128)(2,1)} %bitcast.211, bf16[512,4096]{1,0:T(8,128)(2,1)} %all-gather.2.cloned.1.call-done.weighted_ref), custom_call_target="tpu_custom_call" | custom-call | tf_op jit(solution)/shard_map/pallas_call | solution.py:260
  440.7 134.5 %shard_map.66 = f32[50,128,128]{2,1,0:T(8,128)} custom-call(bf16[400,128,128]{2,1,0:T(8,128)(2,1)} %shard_map.65.g_ref), custom_call_target="tpu_custom_call" | custom-call | tf_op jit(solution)/shard_map/pallas_call | solution.py:331
  575.2 4.0 copy.74
  (69 shorter events, 13.8 us)
Async XLA Ops:
  6.5 5.5 copy-start.13
  6.5 356.9 %reduce-scatter.2.cloned.1.call-start = ((), (), s32[]{:S(2)}) async-start(), calls=%async_computation.1 | async-start | bytes 5242880 | tf_op jit(solution)/shard_map/reduce_scatter | solution.py:386
  6.5 290.9 %copy-start.16 = (f32[64]{0:T(128)}, f32[64]{0:T(128)S(1)}, u32[]{:S(2)}) copy-start(f32[64]{0:T(128)S(1)} %multiply_exponential_fusion) | copy-start | bytes 772
  7.4 4.7 copy-start.2
  281.0 7.4 %copy-start.3 = (bf16[512,4096]{1,0:T(8,128)(2,1)S(1)}, bf16[512,4096]{1,0:T(8,128)(2,1)}, u32[]{:S(2)}) copy-start(bf16[512,4096]{1,0:T(8,128)(2,1)} %fusion.2.normed_ref) | copy-start | bytes 12582916
  281.0 7.4 %copy-start.18 = (bf16[4096,768]{1,0:T(8,128)(2,1)S(1)}, bf16[4096,768]{1,0:T(8,128)(2,1)}, u32[]{:S(2)}) copy-start(bf16[4096,768]{1,0:T(8,128)(2,1)} %get-tuple-element.9) | copy-start | bytes 18874372
  288.2 4.8 copy-start.9
  291.8 1.5 copy-start.10
  298.9 5.9 %copy-start.11 = (bf16[512,64]{1,0:T(8,128)(2,1)}, bf16[512,64]{1,0:T(8,128)(2,1)S(1)}, u32[]{:S(2)}) copy-start(bf16[512,64]{1,0:T(8,128)(2,1)S(1)} %get-tuple-element.28) | copy-start | bytes 196612
  299.4 4.5 copy-start.5
  300.6 6.3 %copy-start = (f32[512,512,4]{1,0,2:T(8,128)}, f32[512,512,4]{1,0,2:T(8,128)S(1)}, u32[]{:S(2)}) copy-start(f32[512,512,4]{1,0,2:T(8,128)S(1)} %get-tuple-element.36) | copy-start | bytes 12582916
  302.5 4.4 copy-start.14
  303.9 9.9 %copy-start.4 = (bf16[128,4,512]{2,0,1:T(8,128)(2,1)}, bf16[128,4,512]{2,0,1:T(8,128)(2,1)S(1)}, u32[]{:S(2)}) copy-start(bf16[128,4,512]{2,0,1:T(8,128)(2,1)S(1)} %fusion.30) | copy-start | bytes 1572868
  307.0 4.4 copy-start.7
  311.4 2.4 copy-start.8
  318.7 82.3 %all-gather.2.cloned.1.call-start = ((), (), s32[]{:S(2)}) async-start(), calls=%async_computation.2 | async-start | bytes 5242880 | tf_op jit(solution)/shard_map/all_gather | solution.py:394
  401.0 6.7 %copy-start.1 = (f32[512,512,4]{1,0,2:T(8,128)S(1)}, f32[512,512,4]{1,0,2:T(8,128)}, u32[]{:S(2)}) copy-start(f32[512,512,4]{1,0,2:T(8,128)} %copy-done) | copy-start | bytes 12582916
  401.0 6.7 %copy-start.15 = (f32[4,512]{1,0:T(4,128)S(1)}, f32[4,512]{1,0:T(4,128)}, u32[]{:S(2)}) copy-start(f32[4,512]{1,0:T(4,128)} %copy-done.14) | copy-start | bytes 24580
  407.7 2.7 copy-start.6
  410.4 2.2 copy-start.12
  412.5 2.2 copy-start.17
Sparse Core Ops, SparseCore 0:
  318.8 44.5 reduce-scatter.1
  366.5 34.4 all-gather.1

commit v2 on v1

--- a/solution.py
+++ b/solution.py
@@ -84,11 +84,11 @@
     return out
 
 
-def enter(neighbours):
+def enter(neighbours, axis="fsdp"):
     barrier = pltpu.get_barrier_semaphore()
     for neighbour in neighbours:
         pl.semaphore_signal(
-            barrier, inc=1, device_id={"fsdp": neighbour}, device_id_type=pl.DeviceIdType.MESH
+            barrier, inc=1, device_id={axis: neighbour}, device_id_type=pl.DeviceIdType.MESH
         )
     pl.semaphore_wait(barrier, len(neighbours))
 
@@ -344,6 +344,120 @@
     )(partial_slots)
 
 
+def exchange_kernel(mixed_ref, d_mixed_ref, w_ref, p_ref, curv_ref, weighted_ref, back_ref,
+                    terms, near, pair, far, share, rest, send_sem, recv_sem):
+    me = lax.axis_index("seq")
+    side = lax.rem(me, 2)
+    core = me + 1 - 2 * side
+    across = me + 2 - 4 * lax.rem(lax.div(me, 2), 2)
+    enter((core, across), "seq")
+    length, width = terms.shape
+    half = width // 2
+    chunks = recv_sem.shape[1]
+    rows = length // chunks
+    mine = pl.ds(pl.multiple_of(side * half, half), half)
+    other = pl.ds(pl.multiple_of((1 - side) * half, half), half)
+
+    def block(i):
+        return pl.ds(i * rows, rows)
+
+    def copy(stage, i, here, there, target):
+        return pltpu.make_async_remote_copy(
+            src_ref=here,
+            dst_ref=there,
+            send_sem=send_sem.at[stage, i],
+            recv_sem=recv_sem.at[stage, i],
+            device_id={"seq": target},
+            device_id_type=pl.DeviceIdType.MESH,
+        )
+
+    def terms_of(i):
+        tile = width // 4
+
+        def columns(j, carry):
+            cols = pl.ds(pl.multiple_of(j * tile, tile), tile)
+            terms[block(i), cols] = (
+                jnp.dot(d_mixed_ref[block(i), :], w_ref[:, cols], preferred_element_type=jnp.float32)
+                + jnp.dot(mixed_ref[block(i), :], p_ref[:, cols], preferred_element_type=jnp.float32)
+            ).astype(jnp.bfloat16)
+            return carry
+
+        lax.fori_loop(0, 4, columns, 0)
+
+    first = [copy(0, i, terms.at[block(i), other], near.at[block(i)], core) for i in range(chunks)]
+    second = [copy(1, i, pair.at[block(i)], far.at[block(i)], across) for i in range(chunks)]
+    third = [copy(2, i, share.at[block(i)], rest.at[block(i)], core) for i in range(chunks)]
+
+    def send_pair(i):
+        first[i].wait_recv()
+        pair[block(i)] = (
+            terms[block(i), mine].astype(jnp.float32) + near[block(i)].astype(jnp.float32)
+        ).astype(jnp.bfloat16)
+        second[i].start()
+
+    def send_share(i):
+        second[i].wait_recv()
+        total = pair[block(i)].astype(jnp.float32) + far[block(i)].astype(jnp.float32)
+        share[block(i)] = (curv_ref[block(i), mine].astype(jnp.float32) * total).astype(
+            jnp.bfloat16
+        )
+        third[i].start()
+
+    def finish(i):
+        weighted_ref[block(i), mine] = share[block(i)]
+        third[i].wait_recv()
+        weighted_ref[block(i), other] = rest[block(i)]
+        back_ref[block(i), :] = lax.dot_general(
+            weighted_ref[block(i), :],
+            w_ref[...],
+            (((1,), (1,)), ((), ())),
+            preferred_element_type=jnp.float32,
+        ).astype(jnp.bfloat16)
+
+    for i in range(chunks):
+        terms_of(i)
+        first[i].start()
+        if i > 0:
+            send_pair(i - 1)
+    send_pair(chunks - 1)
+    for i in range(chunks):
+        send_share(i)
+        if i > 0:
+            finish(i - 1)
+    finish(chunks - 1)
+    for one in first + second + third:
+        one.wait_send()
+
+
+def exchange(mixed, d_mixed, w_out, p_out, curvature):
+    length, width = curvature.shape
+    chunks = 4
+    vmem = pl.BlockSpec(memory_space=pltpu.VMEM)
+    half = pltpu.VMEM((length, width // 2), jnp.bfloat16)
+    return pl.pallas_call(
+        exchange_kernel,
+        out_shape=(
+            jax.ShapeDtypeStruct((length, width), jnp.bfloat16),
+            jax.ShapeDtypeStruct(mixed.shape, jnp.bfloat16),
+        ),
+        in_specs=[vmem] * 5,
+        out_specs=(vmem, vmem),
+        scratch_shapes=[
+            pltpu.VMEM((length, width), jnp.bfloat16),
+            half,
+            half,
+            half,
+            half,
+            half,
+            pltpu.SemaphoreType.DMA((3, chunks)),
+            pltpu.SemaphoreType.DMA((3, chunks)),
+        ],
+        compiler_params=pltpu.CompilerParams(
+            collective_id=2, has_side_effects=True, vmem_limit_bytes=VMEM_BYTES
+        ),
+    )(mixed, d_mixed, w_out, p_out, curvature)
+
+
 def local(tokens, norm_gain, curvature, weight_slots, probe_slots, block_counts):
     n_columns = lax.axis_size("seq")
     n_owners = lax.axis_size("fsdp")
@@ -380,22 +494,8 @@
     projected = jnp.dot(normed, w_qkv, preferred_element_type=jnp.float32)
     d_projected = jnp.dot(normed, p_qkv, preferred_element_type=jnp.float32)
     mixed, d_mixed = jax.jvp(inner, (projected,), (d_projected,))
-    tangent = jnp.dot(d_mixed, w_out, preferred_element_type=jnp.float32) + jnp.dot(
-        mixed, p_out, preferred_element_type=jnp.float32
-    )
-    share = lax.psum_scatter(
-        tangent.astype(jnp.bfloat16), "seq", scatter_dimension=1, tiled=True
-    ).astype(jnp.float32)
-    share_width = share.shape[1]
-    curv_share = lax.dynamic_slice_in_dim(
-        curvature[0], lax.axis_index("seq") * share_width, share_width, 1
-    )
-    weighted_share = (curv_share.astype(jnp.float32) * share).astype(jnp.bfloat16)
-    weighted = lax.all_gather(weighted_share, "seq", axis=1, tiled=True)
+    weighted, back_mixed = exchange(mixed, d_mixed, w_out, p_out, curvature[0])
     mixed_again, pullback = jax.vjp(inner, projected)
-    back_mixed = lax.dot_general(
-        weighted, w_out, (((1,), (1,)), ((), ())), preferred_element_type=jnp.float32
-    ).astype(jnp.bfloat16)
     (back_projected,) = pullback(back_mixed)
     partial_slots = gradient_slots(
         slot_of,

time: 590 us -> 561 us (0.951)
  waiting for transfers between devices: 79.3 us -> 0 us
  Pallas kernels: 422 us -> 485 us
  between operations: 14.1 us -> 0.94 us
  matrix products: 41.4 us -> 33 us
    pallas_call x0 -> x1, Pallas kernels: none -> 62.3 us  [exchange(): pl.pallas_call(exchange_kernel, out_shape=(jax.ShapeDtypeStruct((length,...]
    reduce_scatter x1 -> x0, waiting for transfers between devices: 44.6 us -> none  [local(): lax.psum_scatter(tangent.astype(jnp.bfloat16), 'seq', scatter_dimension=1...]
    all_gather x1 -> x0, waiting for transfers between devices: 34.6 us -> none  [local(): weighted = lax.all_gather(weighted_share, 'seq', axis=1, tiled=True)]
    dot_general x3 -> x0, matrix products: 13.2 us -> none  [the longest x1 5.95 us: local(): lax.dot_general(weighted, w_out, (((1,), (1,)), ((), ())), preferred_elem...]
  transfers between devices with their start and end apart: 2 -> 0, of which waited for: 2 -> 0; matrix products, arithmetic and copies ran while one was open for 0% -> 0% of each run, Pallas kernels for 0% -> 0%
where the time goes in v2:
time: 561 us; the launch traced here: 554 us
  Pallas kernels  485 us (86%)
  matrix products  33 us (6%)
  other arithmetic  20.4 us (4%)
  local copies, waits for them, and re-layouts  14.5 us (3%)
    pallas_call x1, Pallas kernels, gather_weights(): pl.pallas_call(functools.partial(gather_kernel, n, slots, grid_qkv, grid_...  265 us
    pallas_call x1, Pallas kernels, reduce_slots(): pl.pallas_call(functools.partial(reduce_kernel, n, slots, scale), out_sha...  135 us
    pallas_call x1, Pallas kernels, exchange(): pl.pallas_call(exchange_kernel, out_shape=(jax.ShapeDtypeStruct((length,...  62.3 us
    pallas_call x1, Pallas kernels, gradient_slots(): pl.pallas_call(functools.partial(gradient_kernel, grid_qkv, grid_out), ou...  22.7 us
    dot_general x5, matrix products, attention(): jnp.einsum('kgqs,skd->qkgd', attn_probs, values, preferred_element_type=j...  12 us

profile of v2, /device:TPU:0, one launch (start us, length us, event | category | flops | bytes accessed | tf_op | source)
XLA Modules:
  0.0 553.8 jit_solution(6418022055751424166)
XLA Ops:
  2.4 3.1 fusion
  5.6 1.7 fusion.60
  7.4 3.6 fusion.2.normed_ref
  10.9 265.3 %shard_map.64 = (bf16[4096,768]{1,0:T(8,128)(2,1)}, bf16[512,4096]{1,0:T(8,128)(2,1)}, bf16[4096,768]{1,0:T(8,128)(2,1)}, bf16[512,4096]{1,0:T(8,128)(2,1)}) custom-call(s32[320]{0:T(512)} %add_subtract_fusion.slot_ref, bf16[50,128,128]{2,1,0:T(8,128)(2,1)} %bitcast.210, bf16[50,128,128]{2,1,0:T(8,128)(2,1)} %bitcast.211), custom_call_target="tpu_custom_call" | custom-call | tf_op jit(solution)/shard_map/pallas_call | solution.py:197
  276.2 7.0 %fusion.88 = f32[512,768]{1,0:T(8,128)S(1)} fusion(bf16[512,4096]{1,0:T(8,128)(2,1)} %fusion.2.normed_ref, bf16[4096,768]{1,0:T(8,128)(2,1)} %get-tuple-element.11), kind=kOutput, calls=%fused_computation.108 | convolution fusion | flops 3221225472 | bytes 12058624 | tf_op jit(solution)/shard_map/dot_general | solution.py:494
  284.9 2.0 fusion.86
  287.9 5.5 %fusion.89 = f32[512,768]{1,0:T(8,128)S(1)} fusion(bf16[512,4096]{1,0:T(8,128)(2,1)S(1)} %copy-done.4, bf16[4096,768]{1,0:T(8,128)(2,1)} %get-tuple-element.12), kind=kOutput, calls=%fused_computation.109 | convolution fusion | flops 3221225472 | bytes 12058624 | tf_op jit(solution)/shard_map/dot_general | solution.py:495
  293.4 1.2 slice_bitcast_fusion
  294.6 2.0 fusion.71
  297.9 2.3 subtract_convert_fusion
  302.5 2.1 fusion.87
  305.5 2.8 fusion.14
  309.2 1.6 fusion.25
  311.9 1.4 fusion.29
  314.3 62.3 %shard_map.65 = (bf16[512,4096]{1,0:T(8,128)(2,1)}, bf16[512,512]{1,0:T(8,128)(2,1)}) custom-call(bf16[512,512]{1,0:T(8,128)(2,1)} %copy.58.mixed_ref, bf16[512,512]{1,0:T(8,128)(2,1)} %copy.82.d_mixed_ref, bf16[512,4096]{1,0:T(8,128)(2,1)} %get-tuple-element.13.w_ref, bf16[512,4096]{1,0:T(8,128)(2,1)} %get-tuple-element.14.p_ref, bf16[512,4096]{1,0:T(8,128)(2,1)} %bitcast.205), custom_call_target="tpu_custom_call" | custom-call | tf_op jit(solution)/shard_map/pallas_call | solution.py:437
  376.7 1.3 copy.83
  377.9 2.3 fusion.47
  380.3 4.0 fusion.11
  384.3 2.1 fusion.53
  386.5 2.1 fusion.28
  388.6 1.4 multiply_add_fusion.3
  391.9 22.7 %shard_map.66.g_ref = bf16[400,128,128]{2,1,0:T(8,128)(2,1)} custom-call(s32[320]{0:T(512)} %add_subtract_fusion.slot_ref, bf16[512,4096]{1,0:T(8,128)(2,1)} %fusion.2.normed_ref, bf16[512,768]{1,0:T(8,128)(2,1)} %add_convert_fusion.2.d_proj_ref, bf16[512,512]{1,0:T(8,128)(2,1)} %bitcast.204, bf16[512,4096]{1,0:T(8,128)(2,1)} %get-tuple-element.16.weighted_ref), custom_call_target="tpu_custom_call" | custom-call | tf_op jit(solution)/shard_map/pallas_call | solution.py:260
  414.6 134.8 %shard_map.67 = f32[50,128,128]{2,1,0:T(8,128)} custom-call(bf16[400,128,128]{2,1,0:T(8,128)(2,1)} %shard_map.66.g_ref), custom_call_target="tpu_custom_call" | custom-call | tf_op jit(solution)/shard_map/pallas_call | solution.py:331
  549.4 4.0 copy.98
  (70 shorter events, 14.3 us)
Async XLA Ops:
  0.0 7.4 %copy-start.16 = (f32[4096]{0:T(1024)S(1)}, f32[4096]{0:T(1024)}, u32[]{:S(2)}) copy-start(f32[4096]{0:T(1024)} %param.7) | copy-start | bytes 49156
  0.0 294.6 %copy-start.19 = (f32[64]{0:T(128)}, f32[64]{0:T(128)S(1)}, u32[]{:S(2)}) copy-start(f32[64]{0:T(128)S(1)} %multiply_exponential_fusion) | copy-start | bytes 772
  0.9 6.5 %copy-start.3 = (bf16[1,512,4096]{2,1,0:T(8,128)(2,1)S(1)}, bf16[1,512,4096]{2,1,0:T(8,128)(2,1)}, u32[]{:S(2)}) copy-start(bf16[1,512,4096]{2,1,0:T(8,128)(2,1)} %param.6) | copy-start | bytes 12582916
  283.3 1.2 copy-start.10
  284.9 2.9 copy-start.4
  293.4 3.2 copy-start.11
  297.9 2.3 copy-start.14
  297.9 2.3 copy-start.15
  300.2 2.2 copy-start.6
  300.2 1.0 copy-start.12
  302.4 5.8 %copy-start = (f32[512,512,4]{1,0,2:T(8,128)}, f32[512,512,4]{1,0,2:T(8,128)S(1)}, u32[]{:S(2)}) copy-start(f32[512,512,4]{1,0,2:T(8,128)S(1)} %get-tuple-element.40) | copy-start | bytes 12582916
  305.5 2.8 copy-start.17
  309.2 2.6 copy-start.2
  313.3 63.4 %copy-start.5 = (bf16[128,4,512]{2,0,1:T(8,128)(2,1)}, bf16[128,4,512]{2,0,1:T(8,128)(2,1)S(1)}, u32[]{:S(2)}) copy-start(bf16[128,4,512]{2,0,1:T(8,128)(2,1)S(1)} %fusion.29) | copy-start | bytes 1572868
  314.3 65.9 %copy-start.18 = (f32[4,512]{1,0:T(4,128)S(1)}, f32[4,512]{1,0:T(4,128)}, u32[]{:S(2)}) copy-start(f32[4,512]{1,0:T(4,128)} %copy-done.17) | copy-start | bytes 24580
  380.2 4.0 copy-start.1
  380.3 4.0 copy-start.7
  384.3 2.2 copy-start.13
  386.4 2.2 copy-start.20
  386.4 3.7 copy-start.8
  386.5 3.7 copy-start.9

commit v3 on v2

--- a/solution.py
+++ b/solution.py
@@ -93,8 +93,9 @@
     pl.semaphore_wait(barrier, len(neighbours))
 
 
-def gather_kernel(n, slots, grid_qkv, grid_out, slot_ref, w_ref, p_ref, wq_ref, wo_ref, pq_ref,
-                  po_ref, held_w, held_p, send_sem, recv_sem):
+def gather_kernel(n, slots, grid_qkv, grid_out, slot_ref, w_ref, p_ref, tokens_ref, gain_ref,
+                  proj_ref, d_proj_ref, wo_ref, po_ref, normed_t_ref, held_w, held_p, matrix,
+                  normed, send_sem, recv_sem):
     me = lax.axis_index("fsdp")
     pos = ring_position(me, n)
     right = ring_index(lax.rem(pos + 1, n), n)
@@ -141,6 +142,40 @@
                 if j < len(parts[direction]):
                     yield direction, j
 
+    def normalize():
+        rows = 32
+
+        def some(i, carry):
+            here = pl.ds(pl.multiple_of(i * rows, rows), rows)
+            values = tokens_ref[here, :].astype(jnp.float32)
+            factor = lax.rsqrt(jnp.mean(values * values, axis=-1, keepdims=True) + EPS)
+            normed[here, :] = (values * factor * gain_ref[...]).astype(jnp.bfloat16)
+            return carry
+
+        lax.fori_loop(0, normed.shape[0] // rows, some, 0)
+
+    def transpose():
+        edge = held_w.shape[-1]
+
+        def some(i, carry):
+            here = pl.ds(pl.multiple_of(i * edge, edge), edge)
+            normed_t_ref[here, :] = normed[:, here].T
+            return carry
+
+        lax.fori_loop(0, normed.shape[1] // edge, some, 0)
+
+    def project(result_ref):
+        rows = 256
+
+        def some(i, carry):
+            here = pl.ds(pl.multiple_of(i * rows, rows), rows)
+            result_ref[here, :] = jnp.dot(
+                normed[here, :], matrix[...], preferred_element_type=jnp.float32
+            )
+            return carry
+
+        lax.fori_loop(0, normed.shape[0] // rows, some, 0)
+
     def unpack(which, qkv_ref, out_ref):
         own, held = arrays[which]
         rows, cols = grid_qkv
@@ -181,37 +216,48 @@
                 one = copy(which, step, direction, j)
                 one.start()
                 sent.append(one)
+            if which == 0 and step == 0:
+                normalize()
+            if which == 0 and step == 1:
+                transpose()
             if which == 1 and step == 0:
-                finish(0, wq_ref, wo_ref)
-    finish(1, pq_ref, po_ref)
+                finish(0, matrix, wo_ref)
+            if which == 1 and step == 1:
+                project(proj_ref)
+    finish(1, matrix, po_ref)
+    project(d_proj_ref)
     for one in sent:
         one.wait_send()
 
 
-def gather_weights(slot_of, weights, probes, n, grid_qkv, grid_out):
+def gather_weights(slot_of, weights, probes, tokens, gain, n, grid_qkv, grid_out):
     slots, edge, _ = weights.shape
     cuts = max(len(part) for part in pieces(slots))
-    qkv = jax.ShapeDtypeStruct((grid_qkv[0] * edge, grid_qkv[1] * edge), jnp.bfloat16)
+    length, width = tokens.shape
+    proj = jax.ShapeDtypeStruct((length, grid_qkv[1] * edge), jnp.float32)
+    turned = jax.ShapeDtypeStruct((width, length), jnp.bfloat16)
     out = jax.ShapeDtypeStruct((grid_out[0] * edge, grid_out[1] * edge), jnp.bfloat16)
     vmem = pl.BlockSpec(memory_space=pltpu.VMEM)
     return pl.pallas_call(
         functools.partial(gather_kernel, n, slots, grid_qkv, grid_out),
-        out_shape=(qkv, out, qkv, out),
-        in_specs=[pl.BlockSpec(memory_space=pltpu.SMEM), vmem, vmem],
-        out_specs=(vmem,) * 4,
+        out_shape=(proj, proj, out, out, turned),
+        in_specs=[pl.BlockSpec(memory_space=pltpu.SMEM)] + [vmem] * 4,
+        out_specs=(vmem,) * 5,
         scratch_shapes=[
             pltpu.VMEM((n * slots, edge, edge), jnp.bfloat16),
             pltpu.VMEM((n * slots, edge, edge), jnp.bfloat16),
+            pltpu.VMEM((grid_qkv[0] * edge, grid_qkv[1] * edge), jnp.bfloat16),
+            pltpu.VMEM((length, width), jnp.bfloat16),
             pltpu.SemaphoreType.DMA((2, n - 1, 2, cuts)),
             pltpu.SemaphoreType.DMA((2, n - 1, 2, cuts)),
         ],
         compiler_params=pltpu.CompilerParams(
             collective_id=0, has_side_effects=True, vmem_limit_bytes=VMEM_BYTES
         ),
-    )(slot_of, weights, probes)
-
-
-def gradient_kernel(grid_qkv, grid_out, slot_ref, normed_ref, d_proj_ref, mixed_t_ref,
+    )(slot_of, weights, probes, tokens, gain)
+
+
+def gradient_kernel(grid_qkv, grid_out, slot_ref, normed_t_ref, d_proj_ref, mixed_t_ref,
                     weighted_ref, out_ref):
     edge = out_ref.shape[-1]
     rows, cols = grid_qkv
@@ -226,9 +272,9 @@
 
     def qkv_rows(i, carry):
         width = group * edge
-        left = normed_ref[:, pl.ds(pl.multiple_of(i * width, width), width)]
-        block = lax.dot_general(
-            left, d_proj_ref[...], (((0,), (0,)), ((), ())), preferred_element_type=jnp.float32
+        left = normed_t_ref[pl.ds(pl.multiple_of(i * width, width), width), :]
+        block = jnp.dot(
+            left, d_proj_ref[...], preferred_element_type=jnp.float32
         ).astype(jnp.bfloat16)
         for r in range(group):
             for c in range(cols):
@@ -255,7 +301,7 @@
     lax.fori_loop(0, out_cols // group, out_columns, 0)
 
 
-def gradient_slots(slot_of, normed, d_proj, mixed_t, weighted, total_slots, grid_qkv, grid_out):
+def gradient_slots(slot_of, normed_t, d_proj, mixed_t, weighted, total_slots, grid_qkv, grid_out):
     vmem = pl.BlockSpec(memory_space=pltpu.VMEM)
     return pl.pallas_call(
         functools.partial(gradient_kernel, grid_qkv, grid_out),
@@ -263,7 +309,7 @@
         in_specs=[pl.BlockSpec(memory_space=pltpu.SMEM)] + [vmem] * 4,
         out_specs=vmem,
         compiler_params=pltpu.CompilerParams(vmem_limit_bytes=VMEM_BYTES),
-    )(slot_of, normed, d_proj, mixed_t, weighted)
+    )(slot_of, normed_t, d_proj, mixed_t, weighted)
 
 
 def reduce_kernel(n, slots, scale, g_ref, out_ref, held, send_sem, recv_sem):
@@ -480,26 +526,28 @@
         jnp.where(owners[:, None] == owner_ids[None, :], starts[None, :], 0), axis=1
     )
     slot_of = (owners * slots + block_ids - first_block).astype(jnp.int32)
-    w_qkv, w_out, p_qkv, p_out = gather_weights(
-        slot_of, weight_slots[0], probe_slots[0], n_owners, grid_qkv, grid_out
-    )
-    values = tokens[0].astype(jnp.float32)
-    factor = lax.rsqrt(jnp.mean(values * values, axis=-1, keepdims=True) + EPS)
-    normed = (values * factor * norm_gain).astype(jnp.bfloat16)
+    projected, d_projected, w_out, p_out, normed_t = gather_weights(
+        slot_of,
+        weight_slots[0],
+        probe_slots[0],
+        tokens[0],
+        norm_gain[None, :],
+        n_owners,
+        grid_qkv,
+        grid_out,
+    )
     cosine, sine = rotary(length, HD)
 
     def inner(projected):
         return attention(projected, cosine, sine, q_heads, kv_heads)
 
-    projected = jnp.dot(normed, w_qkv, preferred_element_type=jnp.float32)
-    d_projected = jnp.dot(normed, p_qkv, preferred_element_type=jnp.float32)
     mixed, d_mixed = jax.jvp(inner, (projected,), (d_projected,))
     weighted, back_mixed = exchange(mixed, d_mixed, w_out, p_out, curvature[0])
     mixed_again, pullback = jax.vjp(inner, projected)
     (back_projected,) = pullback(back_mixed)
     partial_slots = gradient_slots(
         slot_of,
-        normed,
+        normed_t,
         back_projected.astype(jnp.bfloat16),
         mixed_again.T,
         weighted,

time: 561 us -> 539 us (0.961)
  matrix products: 33 us -> 20.4 us
  other arithmetic: 20.4 us -> 11.8 us
    dot_general x2 -> x0, matrix products: 12.6 us -> none  [the longest x1 7.05 us: local(): projected = jnp.dot(normed, w_qkv, preferred_element_type=jnp.float32)]
where the time goes in v3:
time: 539 us; the launch traced here: 534 us
  Pallas kernels  487 us (90%)
  matrix products  20.4 us (4%)
  local copies, waits for them, and re-layouts  13.3 us (2%)
  other arithmetic  11.8 us (2%)
    pallas_call x1, Pallas kernels, gather_weights(): pl.pallas_call(functools.partial(gather_kernel, n, slots, grid_qkv, grid_...  269 us
    pallas_call x1, Pallas kernels, reduce_slots(): pl.pallas_call(functools.partial(reduce_kernel, n, slots, scale), out_sha...  135 us
    pallas_call x1, Pallas kernels, exchange(): pl.pallas_call(exchange_kernel, out_shape=(jax.ShapeDtypeStruct((length,...  62.3 us
    pallas_call x1, Pallas kernels, gradient_slots(): pl.pallas_call(functools.partial(gradient_kernel, grid_qkv, grid_out), ou...  21.9 us
    dot_general x5, matrix products, attention(): jnp.einsum('kgqs,skd->qkgd', attn_probs, values, preferred_element_type=j...  12 us

profile of v3, /device:TPU:0, one launch (start us, length us, event | category | flops | bytes accessed | tf_op | source)
XLA Modules:
  0.0 533.8 jit_solution(2253116330762996687)
XLA Ops:
  2.4 1.7 fusion.57
  4.1 268.5 %shard_map.64 = (f32[512,768]{1,0:T(8,128)}, f32[512,768]{1,0:T(8,128)}, bf16[512,4096]{1,0:T(8,128)(2,1)}, bf16[512,4096]{1,0:T(8,128)(2,1)}, bf16[4096,512]{1,0:T(8,128)(2,1)}) custom-call(s32[320]{0:T(512)} %add_subtract_fusion.slot_ref, bf16[50,128,128]{2,1,0:T(8,128)(2,1)} %bitcast.203, bf16[50,128,128]{2,1,0:T(8,128)(2,1)} %bitcast.204, ...), custom_call_target="tpu_custom_call" | custom-call | tf_op jit(solution)/shard_map/pallas_call | solution.py:241
  272.6 1.1 slice_bitcast_fusion
  273.7 2.0 fusion.68
  275.7 1.3 slice.62
  277.4 1.3 slice.55
  279.1 1.2 fusion.82
  282.0 1.2 fusion.10
  283.2 2.1 fusion.84
  286.3 2.8 fusion.11
  290.0 1.6 fusion.22
  291.6 1.0 copy.62.d_mixed_ref
  292.7 1.4 fusion.26
  294.1 1.0 copy.38.mixed_ref
  295.1 62.3 %shard_map.65 = (bf16[512,4096]{1,0:T(8,128)(2,1)}, bf16[512,512]{1,0:T(8,128)(2,1)}) custom-call(bf16[512,512]{1,0:T(8,128)(2,1)} %copy.38.mixed_ref, bf16[512,512]{1,0:T(8,128)(2,1)} %copy.62.d_mixed_ref, bf16[512,4096]{1,0:T(8,128)(2,1)} %get-tuple-element.15.w_ref, bf16[512,4096]{1,0:T(8,128)(2,1)} %get-tuple-element.16.p_ref, bf16[512,4096]{1,0:T(8,128)(2,1)} %bitcast.199), custom_call_target="tpu_custom_call" | custom-call | tf_op jit(solution)/shard_map/pallas_call | solution.py:483
  357.4 1.3 copy.63
  358.7 2.3 fusion.44
  361.0 4.0 fusion.8
  365.0 2.1 fusion.50
  367.2 2.1 fusion.25
  369.4 1.4 multiply_add_fusion.3
  372.7 21.9 %shard_map.66.g_ref = bf16[400,128,128]{2,1,0:T(8,128)(2,1)} custom-call(s32[320]{0:T(512)} %add_subtract_fusion.slot_ref, bf16[4096,512]{1,0:T(8,128)(2,1)} %get-tuple-element.12.normed_t_ref, bf16[512,768]{1,0:T(8,128)(2,1)} %add_convert_fusion.2.d_proj_ref, bf16[512,512]{1,0:T(8,128)(2,1)} %bitcast.197, bf16[512,4096]{1,0:T(8,128)(2,1)} %get-tuple-element.18.weighted_ref), custom_call_target="tpu_custom_call" | custom-call | tf_op jit(solution)/shard_map/pallas_call | solution.py:306
  394.6 134.8 %shard_map.67 = f32[50,128,128]{2,1,0:T(8,128)} custom-call(bf16[400,128,128]{2,1,0:T(8,128)(2,1)} %shard_map.66.g_ref), custom_call_target="tpu_custom_call" | custom-call | tf_op jit(solution)/shard_map/pallas_call | solution.py:377
  529.3 4.0 copy.82
  (56 shorter events, 8.7 us)
Async XLA Ops:
  0.0 273.7 %copy-start.16 = (f32[64]{0:T(128)}, f32[64]{0:T(128)S(1)}, u32[]{:S(2)}) copy-start(f32[64]{0:T(128)S(1)} %multiply_exponential_fusion) | copy-start | bytes 772
  279.0 1.3 copy-start.6
  279.0 1.3 copy-start.8
  280.3 0.9 copy-start.12
  280.3 1.0 copy-start.13
  280.9 2.4 copy-start.4
  280.9 1.2 copy-start.10
  283.2 5.8 %copy-start = (f32[512,512,4]{1,0,2:T(8,128)}, f32[512,512,4]{1,0,2:T(8,128)S(1)}, u32[]{:S(2)}) copy-start(f32[512,512,4]{1,0,2:T(8,128)S(1)} %get-tuple-element.42) | copy-start | bytes 12582916
  286.2 2.8 copy-start.14
  290.0 2.6 copy-start.2
  294.1 63.3 %copy-start.3 = (bf16[128,4,512]{2,0,1:T(8,128)(2,1)}, bf16[128,4,512]{2,0,1:T(8,128)(2,1)S(1)}, u32[]{:S(2)}) copy-start(bf16[128,4,512]{2,0,1:T(8,128)(2,1)S(1)} %fusion.26) | copy-start | bytes 1572868
  295.1 65.9 %copy-start.15 = (f32[4,512]{1,0:T(4,128)S(1)}, f32[4,512]{1,0:T(4,128)}, u32[]{:S(2)}) copy-start(f32[4,512]{1,0:T(4,128)} %copy-done.14) | copy-start | bytes 24580
  361.0 4.0 copy-start.1
  361.0 4.0 copy-start.5
  365.0 2.2 copy-start.11
  367.2 2.2 copy-start.17
  367.2 3.7 copy-start.7
  367.2 3.7 copy-start.9

commit v4 on v3

--- a/solution.py
+++ b/solution.py
@@ -257,18 +257,14 @@
     )(slot_of, weights, probes, tokens, gain)
 
 
-def gradient_kernel(grid_qkv, grid_out, slot_ref, normed_t_ref, d_proj_ref, mixed_t_ref,
-                    weighted_ref, out_ref):
+def gradient_blocks(grid_qkv, grid_out, normed_t_ref, d_proj_ref, mixed_t_ref, weighted_ref,
+                    out_ref):
     edge = out_ref.shape[-1]
     rows, cols = grid_qkv
     out_rows, out_cols = grid_out
     group = 2
 
-    def clear(i, carry):
-        out_ref[i] = jnp.zeros(out_ref.shape[1:], out_ref.dtype)
-        return carry
-
-    lax.fori_loop(0, out_ref.shape[0], clear, 0)
+    out_ref[rows * cols + out_rows * out_cols] = jnp.zeros((edge, edge), out_ref.dtype)
 
     def qkv_rows(i, carry):
         width = group * edge
@@ -278,7 +274,7 @@
         ).astype(jnp.bfloat16)
         for r in range(group):
             for c in range(cols):
-                out_ref[slot_ref[(i * group + r) * cols + c]] = block[
+                out_ref[(i * group + r) * cols + c] = block[
                     r * edge:(r + 1) * edge, c * edge:(c + 1) * edge
                 ]
         return carry
@@ -293,7 +289,7 @@
         ).astype(jnp.bfloat16)
         for r in range(out_rows):
             for c in range(group):
-                out_ref[slot_ref[rows * cols + r * out_cols + i * group + c]] = block[
+                out_ref[rows * cols + r * out_cols + i * group + c] = block[
                     r * edge:(r + 1) * edge, c * edge:(c + 1) * edge
                 ]
         return carry
@@ -301,18 +297,8 @@
     lax.fori_loop(0, out_cols // group, out_columns, 0)
 
 
-def gradient_slots(slot_of, normed_t, d_proj, mixed_t, weighted, total_slots, grid_qkv, grid_out):
-    vmem = pl.BlockSpec(memory_space=pltpu.VMEM)
-    return pl.pallas_call(
-        functools.partial(gradient_kernel, grid_qkv, grid_out),
-        out_shape=jax.ShapeDtypeStruct((total_slots, BLK, BLK), jnp.bfloat16),
-        in_specs=[pl.BlockSpec(memory_space=pltpu.SMEM)] + [vmem] * 4,
-        out_specs=vmem,
-        compiler_params=pltpu.CompilerParams(vmem_limit_bytes=VMEM_BYTES),
-    )(slot_of, normed_t, d_proj, mixed_t, weighted)
-
-
-def reduce_kernel(n, slots, scale, g_ref, out_ref, held, send_sem, recv_sem):
+def reduce_kernel(n, slots, scale, grid_qkv, grid_out, pick_ref, normed_t_ref, d_proj_ref,
+                  mixed_t_ref, weighted_ref, out_ref, grads, begin, held, send_sem, recv_sem):
     me = lax.axis_index("fsdp")
     pos = ring_position(me, n)
     right = ring_index(lax.rem(pos + 1, n), n)
@@ -320,16 +306,27 @@
     towards = (right, left)
     enter((left, right))
     parts = pieces(slots)
+    gradient_blocks(
+        grid_qkv, grid_out, normed_t_ref, d_proj_ref, mixed_t_ref, weighted_ref, grads
+    )
 
     def own(step, direction, j):
-        first, size = parts[direction][j]
         shift = n - 1 - step if direction == 0 else 1 + step
         target = ring_index(lax.rem(pos + shift, n), n)
-        return pl.ds(target * slots + first, size)
+        return target * slots
+
+    def each_block(direction, j, body):
+        first, size = parts[direction][j]
+
+        def some(i, carry):
+            body(first + i)
+            return carry
+
+        lax.fori_loop(0, size, some, 0)
 
     def copy(step, direction, j):
         first, size = parts[direction][j]
-        here = g_ref.at[own(0, direction, j)] if step == 0 else held.at[step - 1, pl.ds(first, size)]
+        here = begin.at[pl.ds(first, size)] if step == 0 else held.at[step - 1, pl.ds(first, size)]
         return pltpu.make_async_remote_copy(
             src_ref=here,
             dst_ref=held.at[step, pl.ds(first, size)],
@@ -349,37 +346,55 @@
     for step in range(n - 1):
         for direction, j in each():
             first, size = parts[direction][j]
+            base = own(step, direction, j)
             if step > 0:
                 sent[step - 1, direction, j].wait_recv()
-                held[step - 1, pl.ds(first, size)] = (
-                    held[step - 1, pl.ds(first, size)].astype(jnp.float32)
-                    + g_ref[own(step, direction, j)].astype(jnp.float32)
-                ).astype(jnp.bfloat16)
+
+                def add(t, step=step, base=base):
+                    held[step - 1, t] = (
+                        held[step - 1, t].astype(jnp.float32)
+                        + grads[pick_ref[base + t]].astype(jnp.float32)
+                    ).astype(jnp.bfloat16)
+
+                each_block(direction, j, add)
+            else:
+
+                def fill(t, base=base):
+                    begin[t] = grads[pick_ref[base + t]]
+
+                each_block(direction, j, fill)
             one = copy(step, direction, j)
             one.start()
             sent[step, direction, j] = one
     for direction, j in each():
         first, size = parts[direction][j]
         sent[n - 2, direction, j].wait_recv()
-        out_ref[pl.ds(first, size)] = (
-            held[n - 2, pl.ds(first, size)].astype(jnp.float32)
-            + g_ref[own(n - 1, direction, j)].astype(jnp.float32)
-        ) * scale
+        base = own(n - 1, direction, j)
+
+        def last(t, base=base):
+            out_ref[t] = (
+                held[n - 2, t].astype(jnp.float32) + grads[pick_ref[base + t]].astype(jnp.float32)
+            ) * scale
+
+        each_block(direction, j, last)
     for one in sent.values():
         one.wait_send()
 
 
-def reduce_slots(partial_slots, n, scale):
-    total, edge, _ = partial_slots.shape
-    slots = total // n
+def reduce_slots(picked, normed_t, d_proj, mixed_t, weighted, n, scale, grid_qkv, grid_out):
+    slots = picked.shape[0] // n
+    edge = BLK
+    total_blocks = grid_qkv[0] * grid_qkv[1] + grid_out[0] * grid_out[1]
     cuts = max(len(part) for part in pieces(slots))
     vmem = pl.BlockSpec(memory_space=pltpu.VMEM)
     return pl.pallas_call(
-        functools.partial(reduce_kernel, n, slots, scale),
+        functools.partial(reduce_kernel, n, slots, scale, grid_qkv, grid_out),
         out_shape=jax.ShapeDtypeStruct((slots, edge, edge), jnp.float32),
-        in_specs=[vmem],
+        in_specs=[pl.BlockSpec(memory_space=pltpu.SMEM)] + [vmem] * 4,
         out_specs=vmem,
         scratch_shapes=[
+            pltpu.VMEM((total_blocks + 1, edge, edge), jnp.bfloat16),
+            pltpu.VMEM((slots, edge, edge), jnp.bfloat16),
             pltpu.VMEM((n - 1, slots, edge, edge), jnp.bfloat16),
             pltpu.SemaphoreType.DMA((n - 1, 2, cuts)),
             pltpu.SemaphoreType.DMA((n - 1, 2, cuts)),
@@ -387,7 +402,7 @@
         compiler_params=pltpu.CompilerParams(
             collective_id=1, has_side_effects=True, vmem_limit_bytes=VMEM_BYTES
         ),
-    )(partial_slots)
+    )(picked, normed_t, d_proj, mixed_t, weighted)
 
 
 def exchange_kernel(mixed_ref, d_mixed_ref, w_ref, p_ref, curv_ref, weighted_ref, back_ref,
@@ -545,17 +560,23 @@
     weighted, back_mixed = exchange(mixed, d_mixed, w_out, p_out, curvature[0])
     mixed_again, pullback = jax.vjp(inner, projected)
     (back_projected,) = pullback(back_mixed)
-    partial_slots = gradient_slots(
-        slot_of,
+    slot_index = jnp.arange(n_owners * slots, dtype=jnp.int32)
+    place = slot_index % slots
+    owner_hot = (slot_index // slots)[:, None] == owner_ids[None, :]
+    owner_first = jnp.sum(jnp.where(owner_hot, starts[None, :], 0), axis=1)
+    own_count = jnp.sum(jnp.where(owner_hot, counts[None, :], 0), axis=1)
+    picked = jnp.where(place < own_count, owner_first + place, total_blocks).astype(jnp.int32)
+    scaled = reduce_slots(
+        picked,
         normed_t,
         back_projected.astype(jnp.bfloat16),
         mixed_again.T,
         weighted,
-        n_owners * slots,
+        n_owners,
+        (length * n_owners) ** -0.5,
         grid_qkv,
         grid_out,
     )
-    scaled = reduce_slots(partial_slots, n_owners, (length * n_owners) ** -0.5)
     return scaled.reshape(1, slots, BLK, BLK)
 
 

time: 539 us -> 521 us (0.967)
  Pallas kernels: 487 us -> 476 us
    pallas_call x2 -> x1, Pallas kernels: 157 us -> 145 us  [reduce_slots(): pl.pallas_call(functools.partial(reduce_kernel, n, slots, scale, grid_qkv...]
where the time goes in v4:
time: 521 us
  Pallas kernels  476 us (91%)
  matrix products  20.4 us (4%)
  local copies, waits for them, and re-layouts  13.1 us (3%)
  other arithmetic  11.1 us (2%)
    pallas_call x1, Pallas kernels, gather_weights(): pl.pallas_call(functools.partial(gather_kernel, n, slots, grid_qkv, grid_...  268 us
    pallas_call x1, Pallas kernels, reduce_slots(): pl.pallas_call(functools.partial(reduce_kernel, n, slots, scale, grid_qkv...  145 us
    pallas_call x1, Pallas kernels, exchange(): pl.pallas_call(exchange_kernel, out_shape=(jax.ShapeDtypeStruct((length,...  62.3 us
    dot_general x5, matrix products, attention(): jnp.einsum('kgqs,skd->qkgd', attn_probs, values, preferred_element_type=j...  12 us

profile of v4, /device:TPU:0, one launch (start us, length us, event | category | flops | bytes accessed | tf_op | source)
XLA Modules:
  0.0 520.8 jit_solution(1161910811117251182)
XLA Ops:
  2.3 268.5 %shard_map.64 = (f32[512,768]{1,0:T(8,128)}, f32[512,768]{1,0:T(8,128)}, bf16[512,4096]{1,0:T(8,128)(2,1)}, bf16[512,4096]{1,0:T(8,128)(2,1)}, bf16[4096,512]{1,0:T(8,128)(2,1)}) custom-call(s32[320]{0:T(512)} %add_subtract_fusion.slot_ref, bf16[50,128,128]{2,1,0:T(8,128)(2,1)} %bitcast.204, bf16[50,128,128]{2,1,0:T(8,128)(2,1)} %bitcast.205, ...), custom_call_target="tpu_custom_call" | custom-call | tf_op jit(solution)/shard_map/pallas_call | solution.py:241
  270.7 1.3 slice.55
  272.4 1.3 slice.62
  274.0 1.2 fusion.88
  275.3 1.0 fusion.57
  276.8 1.3 slice_bitcast_fusion
  278.1 1.4 fusion.68
  280.4 1.2 fusion.10
  281.6 2.1 fusion.90
  284.7 2.8 fusion.11
  287.4 1.0 divide_convert_fusion
  288.4 1.6 fusion.22
  290.0 1.0 copy.62.d_mixed_ref
  291.1 1.4 fusion.26
  292.5 1.0 copy.38.mixed_ref
  293.5 62.3 %shard_map.65 = (bf16[512,4096]{1,0:T(8,128)(2,1)}, bf16[512,512]{1,0:T(8,128)(2,1)}) custom-call(bf16[512,512]{1,0:T(8,128)(2,1)} %copy.38.mixed_ref, bf16[512,512]{1,0:T(8,128)(2,1)} %copy.62.d_mixed_ref, bf16[512,4096]{1,0:T(8,128)(2,1)} %get-tuple-element.15.w_ref, bf16[512,4096]{1,0:T(8,128)(2,1)} %get-tuple-element.16.p_ref, bf16[512,4096]{1,0:T(8,128)(2,1)} %bitcast.200), custom_call_target="tpu_custom_call" | custom-call | tf_op jit(solution)/shard_map/pallas_call | solution.py:498
  355.8 1.3 copy.63
  357.1 2.3 fusion.44
  359.4 4.0 fusion.8
  363.4 2.1 fusion.50
  365.6 1.4 multiply_add_fusion.3
  367.2 2.1 fusion.25
  371.8 145.0 %shard_map.66 = f32[50,128,128]{2,1,0:T(8,128)} custom-call(s32[400]{0:T(512)} %add_select_fusion.2.pick_ref, bf16[4096,512]{1,0:T(8,128)(2,1)} %get-tuple-element.12.normed_t_ref, bf16[512,768]{1,0:T(8,128)(2,1)} %add_convert_fusion.2.d_proj_ref, bf16[512,512]{1,0:T(8,128)(2,1)} %bitcast.198, bf16[512,4096]{1,0:T(8,128)(2,1)} %get-tuple-element.18.weighted_ref), custom_call_target="tpu_custom_call" | custom-call | tf_op jit(solution)/shard_map/pallas_call | solution.py:390
  516.8 4.0 copy.82
  (60 shorter events, 8.0 us)
Async XLA Ops:
  1.6 0.7 copy-start.16
  275.3 2.8 copy-start.14
  276.3 3.2 copy-start.6
  276.3 3.2 copy-start.8
  276.8 3.6 copy-start.4
  279.5 2.1 copy-start.10
  281.6 5.8 %copy-start = (f32[512,512,4]{1,0,2:T(8,128)}, f32[512,512,4]{1,0,2:T(8,128)S(1)}, u32[]{:S(2)}) copy-start(f32[512,512,4]{1,0,2:T(8,128)S(1)} %get-tuple-element.44) | copy-start | bytes 12582916
  284.6 2.8 copy-start.12
  288.4 5.1 copy-start.2
  292.5 63.3 %copy-start.3 = (bf16[128,4,512]{2,0,1:T(8,128)(2,1)}, bf16[128,4,512]{2,0,1:T(8,128)(2,1)S(1)}, u32[]{:S(2)}) copy-start(bf16[128,4,512]{2,0,1:T(8,128)(2,1)S(1)} %fusion.26) | copy-start | bytes 1572868
  293.5 65.9 %copy-start.13 = (f32[4,512]{1,0:T(4,128)S(1)}, f32[4,512]{1,0:T(4,128)}, u32[]{:S(2)}) copy-start(f32[4,512]{1,0:T(4,128)} %copy-done.12) | copy-start | bytes 24580
  359.4 4.0 copy-start.1
  359.4 4.0 copy-start.5
  363.4 2.2 copy-start.15
  363.4 3.7 copy-start.11
  367.1 2.2 copy-start.7
  367.1 2.2 copy-start.9
  369.3 1.8 copy-start.17
  369.3 1.8 copy-start.18
